TPU v7x, 32 devices: a whole 2x2x4 slice. The times are simulated.
32 devices in a mesh: row: 2 (over y), col: 4 (over z), depth: 4 (over x, core).
Axes of the slice: x: 2, y: 2, z: 4, core: 2. Of those that a mesh axis runs over, the one named last changes fastest.
Arguments:
- matrix: float32 [8, 2, 512, 8192], P(None, 'row', None, ('col', 'depth')), as said below
Outputs:
- factored: float32 [8, 2, 512, 8192], P(None, 'row', None, ('col', 'depth'))
Inputs may be any that keep to these rules, and one draw needn't show every extreme that they name: matrix is symmetric positive definite.
All inputs are finite; a program needn't handle non-finite values.
Results may differ from a plain program's by a relative error of at most 0.0001.
Values sent between devices are 32-bit elements; how exact they have to be, the bound alone decides.
A program may use at most 128 MiB of HBM per device.

v0:
```python
import functools

import jax
import jax.numpy as jnp
from jax import lax
from jax.experimental import pallas as pl
from jax.experimental.pallas import tpu as pltpu
from jax.sharding import PartitionSpec as P

PANELS = 2
MESH = pl.DeviceIdType.MESH
HI = lax.Precision.HIGHEST
T = 128
NT = (((1,), (1,)), ((), ()))
TN = (((0,), (0,)), ((), ()))
NN = (((1,), (0,)), ((), ()))
DIAGS = ((0, 0), (0, 1), (1, 1))


def dot(a, b, dims=NN):
    return lax.dot_general(a, b, dims, precision=HI, preferred_element_type=jnp.float32)


def factor_tile(aug, tick):
    def strip(i, carry):
        j0 = pl.multiple_of(i * 8, 8)
        rows = aug[pl.ds(j0, 8), :]
        lane = lax.broadcasted_iota(jnp.int32, (8, T), 1)
        sub = lax.broadcasted_iota(jnp.int32, (8, T), 0)
        sub2 = lax.broadcasted_iota(jnp.int32, (8, 2 * T), 0)
        left = rows[:, :T]
        cols = [
            jnp.broadcast_to(
                jnp.sum(jnp.where(lane == j0 + t, left, 0.0), axis=1, keepdims=True), (8, T)
            )
            for t in range(8)
        ]
        for t in range(8):
            p = cols[t][t : t + 1, :]
            r = lax.rsqrt(p)
            r = r * (1.5 - 0.5 * p * r * r)
            coef = cols[t] * r
            for u in range(t + 1, 8):
                head = cols[u][t : t + 1, :] * r
                cols[u] = jnp.where(sub > t, cols[u] - coef * head, cols[u])
            wide_r = jnp.concatenate([r, r], axis=1)
            wide_c = jnp.concatenate([coef, coef], axis=1)
            head = rows[t : t + 1, :] * wide_r
            rows = jnp.where(sub2 == t, head, jnp.where(sub2 > t, rows - wide_c * head, rows))
        aug[pl.ds(j0, 8), :] = rows
        later = jnp.where(lane >= j0 + 8, rows[:, :T], 0.0)
        aug[...] -= dot(later, rows, TN)

        @pl.when(lax.rem(i, 4) == 3)
        def _():
            tick(i // 4)
        return carry

    lax.fori_loop(0, T // 8, strip, 0)


def gather_kernel(
    shape, first, m_ref, x0_ref, x1_ref, cross_ref, w_ref, u_ref,
    diag, work, aug, dsend, drecv, dloc, xsend, xrecv, xloc, csend, crecv, cloc,
):
    n_row, n_col, n_dep = shape
    slots, block, _ = m_ref.shape
    n_chunk = 2 * (slots - first)
    half = block // 2
    r = lax.axis_index("row")
    c = lax.axis_index("col")
    d = lax.axis_index("depth")
    across = lax.rem(d + n_dep // 2, n_dep)
    sib = d + 1 - 2 * lax.rem(d, 2)
    x_refs = (x0_ref, x1_ref)
    n_dc = block // T

    def dest(rr=None, cc=None, dd=None):
        return (r if rr is None else rr, c if cc is None else cc, d if dd is None else dd)

    def role(k):
        is_same = d == k
        is_xp = d == (k + n_dep // 2) % n_dep
        return is_same, is_xp

    def hop_of(k):
        return jnp.where(lax.rem(d, 2) == k % 2, 0, 1)

    def diag_copy(n, g, lane, to):
        part = diag.at[n, pl.ds(g * T, T), :]
        return pltpu.make_async_remote_copy(
            src_ref=part, dst_ref=part, send_sem=dsend.at[n, g, lane], recv_sem=drecv.at[n, g],
            device_id=to, device_id_type=MESH,
        )

    def diag_out(n):
        row, k = DIAGS[n]
        is_same, is_xp = role(k)
        root = is_same & (c == 0) & (r == row)
        out = [
            (is_same & (c < n_col - 1), dest(cc=lax.rem(c + 1, n_col))),
            (is_same, dest(dd=across)),
            (is_same | is_xp, dest(dd=sib)),
        ]
        for step in range(1, n_row):
            out.append((root, dest(rr=lax.rem(r + step, n_row))))
        return root, out

    def diag_load(n, g):
        return pltpu.make_async_copy(
            m_ref.at[0, pl.ds(g * T, T), :], diag.at[n, pl.ds(g * T, T), :], dloc.at[n, g]
        )

    def diag_step(n, g, wait):
        root, out = diag_out(n)

        @pl.when(root)
        def _():
            diag_load(n, g).wait()

        if wait:
            @pl.when(jnp.logical_not(root))
            def _():
                diag_copy(n, g, 0, dest(dd=sib)).wait_recv()

        order = out[3:] + out[:3]
        lanes = list(range(3, len(out))) + [0, 1, 2]
        for lane, (cond, to) in zip(lanes, order):
            @pl.when(cond)
            def _():
                diag_copy(n, g, lane, to).start()

    def diag_drain(n, g):
        _, out = diag_out(n)
        for lane, (cond, to) in enumerate(out):
            @pl.when(cond)
            def _():
                diag_copy(n, g, lane, to).wait_send()

    def x_part(ref, q, shift):
        return ref.at[q // 2 + shift, pl.ds(lax.rem(q, 2) * half, half), :]

    def x_copy(k, q, lane, to, root):
        dst = x_part(x_refs[k], q, 0)
        src = x_part(m_ref, q, first) if root else dst
        return pltpu.make_async_remote_copy(
            src_ref=src, dst_ref=dst, send_sem=xsend.at[k, q, lane], recv_sem=xrecv.at[k, q],
            device_id=to, device_id_type=MESH,
        )

    def x_local(k, q):
        return pltpu.make_async_copy(
            x_part(m_ref, q, first), x_part(x_refs[k], q, 0), xloc.at[k, q]
        )

    def x_out(k, q):
        is_same, is_xp = role(k)
        tree_a = lax.rem(q, 2) == 0
        tree_b = jnp.logical_not(tree_a)
        root = is_same & (c == 0)
        along = (c < n_col - 1) & ((is_same & tree_a) | (is_xp & tree_b))
        side = (
            (is_same & tree_a & (c >= 1))
            | (is_same & tree_b & (c == 0))
            | (is_xp & tree_b & (c >= 1))
        )
        back = is_xp & tree_a & (c == 1)
        return root, [
            (along, dest(cc=lax.rem(c + 1, n_col))),
            (side, dest(dd=across)),
            (is_same | is_xp, dest(dd=sib)),
            (back, dest(cc=jnp.zeros_like(c))),
        ]

    def x_send(k, q, as_root):
        root, out = x_out(k, q)
        for lane, (cond, to) in enumerate(out):
            @pl.when(cond & (root if as_root else jnp.logical_not(root)))
            def _():
                x_copy(k, q, lane, to, as_root).start()

    def tick(t):
        for n in (1, 2):
            row, k = DIAGS[n]
            near = (d - lax.rem(d, 2)) == (k - k % 2)
            hops = c + hop_of(k) + jnp.where(near, 0, 1) + jnp.where(r == row, 0, 1)
            root, _ = diag_out(n)
            e = t - hops
            g = jnp.minimum(jnp.maximum(e, 0), n_dc - 1)

            @pl.when(jnp.logical_not(root) & (e >= 0) & (e < n_dc))
            def _():
                diag_step(n, g, True)
        for k in range(PANELS):
            is_same, is_xp = role(k)
            sib_hop = hop_of(k)
            near = (d - lax.rem(d, 2)) == (k - k % 2)
            for tree in range(2):
                if tree == 0:
                    far = jnp.where(c == 0, 3, c + 1)
                    hops = jnp.where(near, c, far) + sib_hop
                else:
                    back = jnp.where(c == 0, 0, c + 2)
                    hops = jnp.where(near, back, c + 1) + sib_hop
                e = t - 2 * hops
                q = jnp.minimum(jnp.maximum(e, 0), n_chunk - 1)
                root = is_same & (c == 0)
                now = (e >= 0) & (e < n_chunk) & (lax.rem(q, 2) == tree)

                @pl.when(now & jnp.logical_not(root))
                def _():
                    x_copy(k, q, 0, dest(dd=sib), False).wait_recv()
                    x_send(k, q, False)

    def x_drain(q):
        for k in range(PANELS):
            root, out = x_out(k, q)
            for lane, (cond, to) in enumerate(out):
                @pl.when(cond)
                def _():
                    x_copy(k, q, lane, to, False).wait_send()

            @pl.when(root)
            def _():
                x_local(k, q).wait()

    def cross_copy(k, step):
        return pltpu.make_async_remote_copy(
            src_ref=m_ref.at[0], dst_ref=cross_ref.at[k], send_sem=csend.at[k, step - 1],
            recv_sem=crecv.at[k], device_id=dest(rr=lax.rem(r + step, n_row)), device_id_type=MESH,
        )

    def cross_local(k):
        return pltpu.make_async_copy(m_ref.at[0], cross_ref.at[k], cloc.at[k])

    for n, (row, k) in enumerate(DIAGS):
        @pl.when((d == k) & (c == 0) & (r == row))
        def _():
            for g in range(n_dc):
                diag_load(n, g).start()
    for g in range(n_dc):
        diag_step(0, g, True)
    for n in (1, 2):
        root, _ = diag_out(n)

        @pl.when(root)
        def _():
            for g in range(n_dc):
                diag_step(n, g, False)

    def send_all(q, carry):
        for k in range(PANELS):
            x_send(k, q, True)
            root, _ = x_out(k, q)

            @pl.when(root)
            def _():
                x_local(k, q).start()
        return carry

    lax.fori_loop(0, n_chunk, send_all, 0)
    for k in range(PANELS):
        @pl.when(r == k)
        def _():
            cross_local(k).start()
            for step in range(1, n_row):
                cross_copy(k, step).start()

    def eye(rows, columns, at):
        i = lax.broadcasted_iota(jnp.int32, (rows, columns), 0)
        j = lax.broadcasted_iota(jnp.int32, (rows, columns), 1)
        return jnp.where(i + at == j, jnp.float32(1.0), jnp.float32(0.0))

    n_tick = T // 32

    def factor_block(panel):
        def tile(b, carry):
            at = pl.multiple_of(b * T, T)
            aug[:, :T] = work[pl.ds(at, T), pl.ds(at, T)]
            aug[:, T:] = eye(T, T, 0)
            factor_tile(aug, lambda e: tick((panel * n_dc + b) * n_tick + e))
            line = dot(aug[:, T:], work[pl.ds(at, T), :])
            work[pl.ds(at, T), :] = line
            lane = lax.broadcasted_iota(jnp.int32, (T, block), 1)
            aside = jnp.where(lane >= at + T, line[:, :block], 0.0)

            def tail(e, carry2):
                cols = pl.ds(pl.multiple_of(e * 2 * T, 2 * T), 2 * T)
                work[:, cols] -= dot(aside, work[pl.ds(at, T), cols], TN)
                return carry2

            lax.fori_loop(0, block // T, tail, 0)
            return carry

        lax.fori_loop(0, n_dc, tile, 0)

    def upper(x, at):
        i = lax.broadcasted_iota(jnp.int32, x.shape, 0)
        j = lax.broadcasted_iota(jnp.int32, x.shape, 1)
        return jnp.where(i + at <= j, x, 0.0)

    def lower(x, at):
        i = lax.broadcasted_iota(jnp.int32, x.shape, 0)
        j = lax.broadcasted_iota(jnp.int32, x.shape, 1)
        return jnp.where(i + at >= j, x, 0.0)

    def each_tile(f):
        def step(e, carry):
            f(pl.multiple_of(e * T, T))
            return carry

        lax.fori_loop(0, block // T, step, 0)

    def fill(n):
        def f(at):
            rows = pl.ds(at, T)
            work[rows, :block] = diag[n, rows, :]
            work[rows, block:] = eye(T, block, at)
        return f

    def keep(base):
        def f(at):
            rows = pl.ds(at, T)
            to = pl.ds(base + at, T)
            u_ref[to, base : base + block] = upper(work[rows, :block], at)
            w_ref[to, base : base + block] = lower(work[rows, block:], at)
        return f

    each_tile(fill(0))
    factor_block(0)
    each_tile(keep(0))

    def join(at):
        rows = pl.ds(at, T)
        u_ref[rows, block:] = dot(w_ref[rows, :block], diag[1])
        w_ref[rows, block:] = jnp.zeros((T, block), jnp.float32)
        u_ref[pl.ds(block + at, T), :block] = jnp.zeros((T, block), jnp.float32)

    each_tile(join)

    def second(at):
        rows = pl.ds(at, T)
        cols = pl.ds(block + at, T)
        top = u_ref[:block, block:]
        work[rows, :block] = diag[2, rows, :] - dot(u_ref[:block, cols], top, TN)
        work[rows, block:] = eye(T, block, at)

    each_tile(second)
    factor_block(1)
    each_tile(keep(block))

    def below(at):
        rows = pl.ds(at, T)
        cols = pl.ds(block + at, T)
        work[rows, :block] = dot(u_ref[:block, cols], w_ref[:block, :block], TN)

    each_tile(below)

    def corner(at):
        rows = pl.ds(block + at, T)
        w_ref[rows, :block] = -dot(w_ref[rows, block:], work[:, :block])

    each_tile(corner)

    def rest(t, carry):
        tick(t)
        return carry

    lax.fori_loop(PANELS * n_dc * n_tick, max(n_chunk + 2 * (n_col + 2), 32), rest, 0)
    for k in range(PANELS):
        @pl.when(r == k)
        def _():
            cross_local(k).wait()
            for step in range(1, n_row):
                cross_copy(k, step).wait_send()

        @pl.when(r != k)
        def _():
            cross_copy(k, 1).wait_recv()
    for n in range(len(DIAGS)):
        for g in range(n_dc):
            diag_drain(n, g)

    def drain(q, carry):
        x_drain(q)
        return carry

    lax.fori_loop(0, n_chunk, drain, 0)


def split(x):
    top = x.astype(jnp.bfloat16)
    return top, (x - top.astype(jnp.float32)).astype(jnp.bfloat16)


def update_kernel(first, keep_ref, m_ref, x0_ref, x1_ref, mat_ref, fix_ref, o_ref, top, low):
    s = pl.program_id(0)
    block = o_ref.shape[-1]

    @pl.when(s == 0)
    def _():
        for k in range(PANELS):
            a, b = split(mat_ref[k * block : (k + 1) * block, :])
            top[k] = a
            low[k] = b

    def go():
        base = jnp.where(keep_ref[0] > 0, m_ref[0], 0.0)
        acc = base
        for k, x_ref in enumerate((x0_ref, x1_ref)):
            a, b = split(x_ref[0])
            for left, right in ((a, top), (a, low), (b, top)):
                acc = acc - jnp.dot(left, right[k], preferred_element_type=jnp.float32)
        return acc

    if first:
        @pl.when(s == 0)
        def _():
            o_ref[0] = fix_ref[...]

        @pl.when(s > 0)
        def _():
            o_ref[0] = go()
    else:
        o_ref[0] = go()

        @pl.when((s == 0) & (keep_ref[1] > 0))
        def _():
            o_ref[0] = fix_ref[...]


def body(shape, matrix):
    n_row, n_col, n_dep = shape
    m = matrix.reshape(matrix.shape[0], matrix.shape[2], matrix.shape[3])
    slots, block, _ = m.shape
    order = PANELS * block
    first = 1 if n_row <= PANELS else 0
    n_chunk = 2 * (slots - first)
    n_dc = block // T
    f32 = jnp.float32
    dma = pltpu.SemaphoreType.DMA
    hbm = pl.BlockSpec(memory_space=pltpu.HBM)
    vmem = pl.BlockSpec(memory_space=pltpu.VMEM)
    panel = jax.ShapeDtypeStruct((slots - first, block, block), f32)
    x0, x1, cross, w, u = pl.pallas_call(
        functools.partial(gather_kernel, shape, first),
        out_shape=(
            panel, panel,
            jax.ShapeDtypeStruct((PANELS, block, block), f32),
            jax.ShapeDtypeStruct((order, order), f32),
            jax.ShapeDtypeStruct((order, order), f32),
        ),
        in_specs=[hbm],
        out_specs=(hbm, hbm, hbm, vmem, vmem),
        scratch_shapes=[
            pltpu.VMEM((len(DIAGS), block, block), f32),
            pltpu.VMEM((block, 2 * block), f32),
            pltpu.VMEM((T, 2 * T), f32),
            dma((len(DIAGS), n_dc, 2 + n_row)),
            dma((len(DIAGS), n_dc)),
            dma((len(DIAGS), n_dc)),
            dma((PANELS, n_chunk, 4)),
            dma((PANELS, n_chunk)),
            dma((PANELS, n_chunk)),
            dma((PANELS, n_row - 1)),
            dma((PANELS,)),
            dma((PANELS,)),
        ],
        compiler_params=pltpu.CompilerParams(has_side_effects=True, vmem_limit_bytes=48 << 20),
    )(m)

    j = lax.axis_index(("col", "depth"))
    r = lax.axis_index("row")
    own = cross.reshape(order, block)
    solved = jnp.dot(w, own, precision=HI)
    i1 = lax.broadcasted_iota(jnp.int32, (order, block), 0)
    i2 = lax.broadcasted_iota(jnp.int32, (order, block), 1)
    unit = jnp.where(i1 == i2 + j * block, f32(-1.0), f32(0.0))
    mat = lax.dot_general(w, jnp.where(j < PANELS, unit, solved), TN, precision=HI)
    rr = jnp.minimum(r, PANELS - 1)
    jj = jnp.minimum(j, PANELS - 1)
    fix = lax.dynamic_slice(u, (jj * block, rr * block), (block, block)).T
    fix = jnp.where(j < PANELS, fix, f32(0.0))
    flags = jnp.stack([j >= PANELS, r < PANELS]).astype(jnp.int32)

    one = (1, block, block)
    shifted = lambda s: (jnp.maximum(s - first, 0), 0, 0)
    out = pl.pallas_call(
        functools.partial(update_kernel, first),
        out_shape=jax.ShapeDtypeStruct(m.shape, f32),
        grid=(slots,),
        in_specs=[
            pl.BlockSpec(memory_space=pltpu.SMEM),
            pl.BlockSpec(one, lambda s: (s, 0, 0)),
            pl.BlockSpec(one, shifted),
            pl.BlockSpec(one, shifted),
            pl.BlockSpec((order, block), lambda s: (0, 0)),
            pl.BlockSpec((block, block), lambda s: (0, 0)),
        ],
        out_specs=pl.BlockSpec(one, lambda s: (s, 0, 0)),
        scratch_shapes=[
            pltpu.VMEM((PANELS, block, block), jnp.bfloat16),
            pltpu.VMEM((PANELS, block, block), jnp.bfloat16),
        ],
        compiler_params=pltpu.CompilerParams(vmem_limit_bytes=40 << 20),
    )(flags, m, x0, x1, mat, fix)
    return out.reshape(matrix.shape)


def solution(mesh):
    shape = (mesh.shape["row"], mesh.shape["col"], mesh.shape["depth"])
    placed = P(None, "row", None, ("col", "depth"))
    return jax.shard_map(
        functools.partial(body, shape),
        mesh=mesh,
        in_specs=(placed,),
        out_specs=placed,
        check_vma=False,
    )
```

profile of v0, /device:TPU:28, one launch (start us, length us, event | category | flops | bytes accessed | tf_op | source)
XLA Modules:
  0.0 360.4 jit_solution(3327901141988235226)
XLA Ops:
  0.0 0.1 add_convert_fusion.keep_ref
  0.1 318.7 %shard_map.17 = (f32[7,512,512]{2,1,0:T(8,128)}, f32[7,512,512]{2,1,0:T(8,128)}, f32[2,512,512]{2,1,0:T(8,128)S(1)}, f32[1024,1024]{1,0:T(8,128)}, f32[1024,1024]{1,0:T(8,128)}) custom-call(f32[8,512,512]{2,1,0:T(8,128)} %bitcast.15), custom_call_target="tpu_custom_call" | custom-call | tf_op jit(solution)/shard_map/pallas_call | solution.py:445
  318.8 0.0 copy-start.1
  318.8 9.0 %fusion.12 = f32[1024,512]{1,0:T(8,128)S(1)} fusion(f32[1024,1024]{1,0:T(8,128)} %get-tuple-element.12, f32[1024,512]{1,0:T(8,128)S(1)} %bitcast.14), kind=kOutput, calls=%fused_computation.14 | convolution fusion | flops 6442450944 | bytes 8388608 | tf_op jit(solution)/shard_map/dot_general | solution.py:475
  327.7 0.0 copy-done.1
  327.7 6.8 %fusion.3.mat_ref = f32[1024,512]{1,0:T(8,128)S(1)} fusion(f32[1024,1024]{1,0:T(8,128)S(1)} %copy-done.1, f32[1024,512]{1,0:T(8,128)S(1)} %fusion.12, s32[512]{0:T(512)S(1)} %iota_add_fusion, pred[]{:T(512)S(6)} %lt.14), kind=kOutput, calls=%fused_computation.4 | convolution fusion | flops 6444023808 | bytes 8390657 | tf_op jit(solution)/shard_map/dot_general | solution.py:479
  334.6 5.3 %copy.3 = f32[1024,1024]{0,1:T(8,128)} copy(f32[1024,1024]{1,0:T(8,128)} %get-tuple-element.14) | data formatting | bytes 8388608 | tf_op jit(solution)/shard_map/pallas_call | solution.py:445
  339.9 1.3 select_bitcast_fusion.fix_ref
  341.2 0.0 copy-start
  341.3 3.1 copy-done
  344.3 16.1 %shard_map.18 = f32[8,512,512]{2,1,0:T(8,128)} custom-call(s32[2]{0:T(128)S(1)} %add_convert_fusion.keep_ref, f32[8,512,512]{2,1,0:T(8,128)} %bitcast.16, f32[7,512,512]{2,1,0:T(8,128)S(1)} %copy-done, f32[7,512,512]{2,1,0:T(8,128)} %get-tuple-element.11.x1_ref, f32[1024,512]{1,0:T(8,128)S(1)} %fusion.3.mat_ref, f32[512,512]{1,0:T(8,128)S(1)} %select_bitcast_fusion.fix_ref), custom_call_target="tpu_custom_call" | custom-call | tf_op jit(solution)/shard_map/pallas_call | solution.py:488
  (1 shorter events, 0.0 us)
Async XLA Ops:
  318.8 9.0 %copy-start.1 = (f32[1024,1024]{1,0:T(8,128)S(1)}, f32[1024,1024]{1,0:T(8,128)}, u32[]{:S(2)}) copy-start(f32[1024,1024]{1,0:T(8,128)} %get-tuple-element.12) | copy-start | bytes 12582916
  341.2 3.1 copy-start
where the time goes:
time: 361 us; the launch traced here: 360 us
  Pallas kernels  335 us (93%)
  matrix products  15.8 us (4%)
  local copies, waits for them, and re-layouts  8.43 us (2%)
    pallas_call x1, Pallas kernels, body(): pl.pallas_call(functools.partial(gather_kernel, shape, first), out_shape=...  319 us
    pallas_call x1, Pallas kernels, body(): pl.pallas_call(functools.partial(update_kernel, first), out_shape=jax.Sha...  16.1 us
    dot_general x1, matrix products, body(): solved = jnp.dot(w, own, precision=HI)  8.96 us

commit v1 on v0

v1 whole, which is shorter than its diff:
```python
import functools

import jax
import jax.numpy as jnp
from jax import lax
from jax.experimental import pallas as pl
from jax.experimental.pallas import tpu as pltpu
from jax.sharding import PartitionSpec as P

PANELS = 2
MESH = pl.DeviceIdType.MESH
HI = lax.Precision.HIGHEST
T = 128
NT = (((1,), (1,)), ((), ()))
TN = (((0,), (0,)), ((), ()))
NN = (((1,), (0,)), ((), ()))
DIAGS = ((0, 0), (0, 1), (1, 1))


def dot(a, b, dims=NN):
    return lax.dot_general(a, b, dims, precision=HI, preferred_element_type=jnp.float32)


def factor_tile(aug):
    def strip(i, carry):
        j0 = pl.multiple_of(i * 8, 8)
        rows = aug[pl.ds(j0, 8), :]
        lane = lax.broadcasted_iota(jnp.int32, (8, T), 1)
        sub = lax.broadcasted_iota(jnp.int32, (8, T), 0)
        sub2 = lax.broadcasted_iota(jnp.int32, (8, 2 * T), 0)
        left = rows[:, :T]
        cols = [
            jnp.broadcast_to(
                jnp.sum(jnp.where(lane == j0 + t, left, 0.0), axis=1, keepdims=True), (8, T)
            )
            for t in range(8)
        ]
        for t in range(8):
            p = cols[t][t : t + 1, :]
            r = lax.rsqrt(p)
            r = r * (1.5 - 0.5 * p * r * r)
            coef = cols[t] * r
            for u in range(t + 1, 8):
                head = cols[u][t : t + 1, :] * r
                cols[u] = jnp.where(sub > t, cols[u] - coef * head, cols[u])
            wide_r = jnp.concatenate([r, r], axis=1)
            wide_c = jnp.concatenate([coef, coef], axis=1)
            head = rows[t : t + 1, :] * wide_r
            rows = jnp.where(sub2 == t, head, jnp.where(sub2 > t, rows - wide_c * head, rows))
        aug[pl.ds(j0, 8), :] = rows
        later = jnp.where(lane >= j0 + 8, rows[:, :T], 0.0)
        aug[...] -= dot(later, rows, TN)
        return carry

    lax.fori_loop(0, T // 8, strip, 0)


def split(x):
    top = x.astype(jnp.bfloat16)
    return top, (x - top.astype(jnp.float32)).astype(jnp.bfloat16)


def dot3(left, right, dims=NN):
    acc = None
    for a, b in ((left[1], right[0]), (left[0], right[1]), (left[0], right[0])):
        term = lax.dot_general(a, b, dims, preferred_element_type=jnp.float32)
        acc = term if acc is None else acc + term
    return acc


def kernel(
    shape, first, m_ref, o_ref,
    xs, mbuf, diag, work, aug, w, u01, ufix, cross, y0, y1, z0, bt, top, low,
    dsend, drecv, dloc, xsend, xrecv, csend, crecv, cloc, wsend, wrecv, mload, osend,
):
    n_row, n_col, n_dep = shape
    slots, block, _ = m_ref.shape
    held = slots - first
    half = block // 2
    n_dc = block // T
    n_pair = n_dep // 2
    r = lax.axis_index("row")
    c = lax.axis_index("col")
    d = lax.axis_index("depth")
    j = c * n_dep + d
    sib = d + 1 - 2 * lax.rem(d, 2)
    comm = lax.rem(d, 2) == lax.rem(r, 2)
    chain = jnp.logical_not(comm)
    kr = jnp.minimum(r, PANELS - 1)

    def dest(rr=None, cc=None, dd=None):
        return (r if rr is None else rr, c if cc is None else cc, d if dd is None else dd)

    def remote(src, dst, send, recv, to):
        return pltpu.make_async_remote_copy(
            src_ref=src, dst_ref=dst, send_sem=send, recv_sem=recv,
            device_id=to, device_id_type=MESH,
        )

    def chunks(n):
        if n == 1:
            return [(g * T, 0, block) for g in range(n_dc)]
        out = [(g * T, g * T, block - g * T) for g in range(n_dc)]
        if n == 0:
            out[:1] = [(0, 0, T), (0, T, block - T)]
        return out

    def diag_part(ref, n, g):
        at, col, wide = chunks(n)[g]
        return ref.at[pl.ds(at, T), pl.ds(col, wide)]

    def diag_copy(n, g, lane, to):
        part = diag_part(diag.at[n], n, g)
        return remote(part, part, dsend.at[n, g, lane], drecv.at[n, g], to)

    def diag_load(n, g):
        return pltpu.make_async_copy(
            diag_part(m_ref.at[0], n, g), diag_part(diag.at[n], n, g), dloc.at[n, g]
        )

    def diag_roles(n):
        row, k = DIAGS[n]
        root = (r == row) & (c == 0) & (d == k)
        own_entry = row % 2 == k % 2
        near = d < 2
        entry = comm & near & (c == 0) & (r == row)
        out = [(0, comm & near & (c < n_col - 1), dest(cc=lax.rem(c + 1, n_col)))]
        for q in range(1, n_pair):
            out.append((1 + q, comm & near, dest(dd=lax.rem(d + 2 * q, n_dep))))
        for step in range(1, n_row):
            rr = lax.rem(r + step, n_row)
            out.append((n_pair + step, entry, dest(rr=rr, dd=lax.rem(rr, 2))))
        down = comm if own_entry else ((comm & jnp.logical_not(entry)) | root)
        out.insert(0, (1, down, dest(dd=sib)))
        rows = [x for x in out if x[0] > n_pair]
        rest = [x for x in out if x[0] <= n_pair]
        return root, rows + rest

    def diag_step(n, g):
        root, out = diag_roles(n)

        @pl.when(root)
        def _():
            diag_load(n, g).wait()

        @pl.when(jnp.logical_not(root))
        def _():
            diag_copy(n, g, 0, dest(dd=sib)).wait_recv()

        for lane, cond, to in out:
            @pl.when(cond)
            def _():
                diag_copy(n, g, lane, to).start()

    def diag_relay(n):
        for g in range(len(chunks(n))):
            diag_step(n, g)

    def diag_drain(n):
        _, out = diag_roles(n)
        for g in range(len(chunks(n))):
            for lane, cond, to in out:
                @pl.when(cond)
                def _():
                    diag_copy(n, g, lane, to).wait_send()

    def cross_copy(step):
        return remote(
            m_ref.at[0], cross.at[kr], csend.at[step - 1], crecv.at[kr],
            dest(rr=lax.rem(r + step, n_row)),
        )

    def cross_local():
        return pltpu.make_async_copy(m_ref.at[0], cross.at[kr], cloc.at[0])

    def cross_start():
        @pl.when(r < PANELS)
        def _():
            cross_local().start()
            for step in range(1, n_row):
                cross_copy(step).start()

    def cross_wait(k):
        @pl.when(k == r)
        def _():
            cross_local().wait()

        @pl.when(k != r)
        def _():
            remote(
                m_ref.at[0], cross.at[k], csend.at[0], crecv.at[k],
                dest(rr=lax.rem(r + 1, n_row)),
            ).wait_recv()

    def piece(s, side, step):
        cs = c - side * s
        ds = lax.rem(d + 2 * step, n_dep)
        col = jnp.clip(cs, 0, n_col - 1) * n_dep + ds
        a = col // n_row
        ok = comm & (cs >= 0) & (cs < n_col) & (lax.rem(col, n_row) == r) & (a >= first)
        return ok, jnp.clip(a - first, 0, held - 1)

    def piece_out(s, side, step):
        out = []
        if step == 0:
            if side == 1 or s == 0:
                out.append((0, c < n_col - 1, dest(cc=lax.rem(c + 1, n_col))))
            if side == -1 or s == 0:
                out.append((1, c > 0, dest(cc=lax.rem(c + n_col - 1, n_col))))
            for q in range(1, n_pair):
                out.append((2 + q, c >= 0, dest(dd=lax.rem(d + 2 * q, n_dep))))
        out.append((2, c >= 0, dest(dd=sib)))
        return out

    def x_part(k, a, h):
        return xs.at[k, a, pl.ds(pl.multiple_of(h * half, half), half), :]

    def x_copy(k, a, h, lane, to):
        part = x_part(k, a, h)
        return remote(part, part, xsend.at[k, a, h, lane], xrecv.at[k, a, h], to)

    def x_event(s, side, step, k):
        ok, a = piece(s, side, step)

        @pl.when(ok)
        def _():
            def part(h, carry):
                if s > 0 or step > 0:
                    x_copy(k, a, h, 2, dest(dd=sib)).wait_recv()
                for lane, cond, to in piece_out(s, side, step):
                    @pl.when(cond)
                    def _():
                        x_copy(k, a, h, lane, to).start()
                return carry

            lax.fori_loop(0, 2, part, 0)

    places = [(0, 1)] + [(s, side) for s in range(1, n_col) for side in (1, -1)]

    def x_own(k):
        ok, a = piece(0, 1, 0)

        @pl.when(ok)
        def _():
            def turn(e, carry):
                i = pl.multiple_of((e // n_dc) * T, T)
                l = pl.multiple_of(lax.rem(e, n_dc) * T, T)
                xs[k, a, pl.ds(l, T), pl.ds(i, T)] = cross[k, pl.ds(i, T), pl.ds(l, T)].T
                return carry

            lax.fori_loop(0, n_dc * n_dc, turn, 0)

    def x_drain():
        def one(e, carry):
            k = e // 2
            h = lax.rem(e, 2)
            for s, side in places:
                for step in range(n_pair):
                    ok, a = piece(s, side, step)
                    for lane, cond, to in piece_out(s, side, step):
                        @pl.when(ok & cond)
                        def _():
                            x_copy(k, a, h, lane, to).wait_send()
            return carry

        lax.fori_loop(0, 2 * PANELS, one, 0)

    def w_copy(panel, b):
        rows = pl.ds(pl.multiple_of(b * T, T), T)
        part = w.at[panel, rows, :]
        return remote(part, part, wsend.at[panel, b], wrecv.at[panel, b], dest(dd=sib))

    def u_copy():
        return remote(u01, u01, wsend.at[PANELS, 0], wrecv.at[PANELS, 0], dest(dd=sib))

    def fix_copy():
        return remote(ufix, ufix, wsend.at[PANELS, 1], wrecv.at[PANELS, 1], dest(dd=sib))

    def m_load(s):
        return pltpu.make_async_copy(m_ref.at[s + first], mbuf.at[s + first], mload.at[s])

    def all_loads(wait):
        def one(s, carry):
            if wait:
                m_load(s).wait()
            else:
                m_load(s).start()
            return carry

        lax.fori_loop(0, held, one, 0)

    for n, (row, k) in enumerate(DIAGS):
        @pl.when((d == k) & (c == 0) & (r == row))
        def _():
            for g in range(len(chunks(n))):
                diag_load(n, g).start()

    def eye(rows, columns, at):
        i = lax.broadcasted_iota(jnp.int32, (rows, columns), 0)
        l = lax.broadcasted_iota(jnp.int32, (rows, columns), 1)
        return jnp.where(i + at == l, jnp.float32(1.0), jnp.float32(0.0))

    def upper(x, at):
        i = lax.broadcasted_iota(jnp.int32, x.shape, 0)
        l = lax.broadcasted_iota(jnp.int32, x.shape, 1)
        return jnp.where(i + at <= l, x, 0.0)

    def lower(x, at):
        i = lax.broadcasted_iota(jnp.int32, x.shape, 0)
        l = lax.broadcasted_iota(jnp.int32, x.shape, 1)
        return jnp.where(i + at >= l, x, 0.0)

    def each_tile(f, size=T):
        def step(e, carry):
            f(pl.multiple_of(e * size, size))
            return carry

        lax.fori_loop(0, block // size, step, 0)

    @pl.when(comm)
    def _():
        diag_relay(0)
        cross_start()
        for kk in range(PANELS):
            k = lax.rem(r + kk, PANELS)
            cross_wait(k)
            x_own(k)
            for step in range(n_pair):
                x_event(0, 1, step, k)
            diag_relay(1 + kk)
        all_loads(False)
        for s in range(1, n_col):
            for kk in range(PANELS):
                k = lax.rem(r + kk, PANELS)
                for side in (1, -1):
                    for step in range(n_pair):
                        x_event(s, side, step, k)
        for b in range(n_dc):
            w_copy(0, b).wait_recv()
        u_copy().wait_recv()

    def factor_block(panel):
        def tile(b, carry):
            at = pl.multiple_of(b * T, T)
            rows = pl.ds(at, T)
            aug[:, :T] = work[rows, rows]
            aug[:, T:] = eye(T, T, 0)
            factor_tile(aug)
            if panel == 0:
                @pl.when(b == 0)
                def _():
                    for g in range(1, n_dc + 1):
                        diag_step(0, g)
                    each_tile(fill)
            line = dot(aug[:, T:], work[rows, :])
            work[rows, :] = line
            w[panel, rows, :] = lower(line[:, block:], at)

            @pl.when(r == panel)
            def _():
                ufix[rows, :] = upper(line[:, :block], at)

            @pl.when(b < n_dc - 1)
            def _():
                lane = lax.broadcasted_iota(jnp.int32, (T, block), 1)
                aside = jnp.where(lane >= at + T, line[:, :block], 0.0)

                def tail(e, carry2):
                    cols = pl.ds(pl.multiple_of(e * 2 * T, 2 * T), 2 * T)
                    work[:, cols] -= dot(aside, work[rows, cols], TN)
                    return carry2

                lax.fori_loop(0, block // T, tail, 0)

            w_copy(panel, b).start()
            return carry

        lax.fori_loop(0, n_dc, tile, 0)

    def fill(at):
        rows = pl.ds(at, T)
        work[rows, :block] = diag[0, rows, :]
        work[rows, block:] = eye(T, block, at)

    def join(at):
        rows = pl.ds(at, T)
        u01[rows, :] = dot(w[0, rows, :], diag[1])

    def second(at):
        rows = pl.ds(at, T)
        work[rows, :block] = diag[2, rows, :] - dot(u01[:, rows], u01[...], TN)
        work[rows, block:] = eye(T, block, at)

    @pl.when(chain)
    def _():
        cross_start()
        diag_step(0, 0)
        work[pl.ds(0, T), pl.ds(0, T)] = diag[0, pl.ds(0, T), pl.ds(0, T)]
        all_loads(False)
        diag_start = DIAGS[1]

        @pl.when((r == diag_start[0]) & (c == 0) & (d == diag_start[1]))
        def _():
            diag_relay(1)

        factor_block(0)

        @pl.when(jnp.logical_not((r == diag_start[0]) & (c == 0) & (d == diag_start[1])))
        def _():
            diag_relay(1)

        each_tile(join)
        u_copy().start()
        diag_relay(2)
        each_tile(second)
        factor_block(1)
        for k in range(PANELS):
            cross_wait(jnp.int32(k))

        @pl.when(r < PANELS)
        def _():
            fix_copy().start()

    def unit(k, x, at):
        i1 = lax.broadcasted_iota(jnp.int32, x.shape, 0)
        i2 = lax.broadcasted_iota(jnp.int32, x.shape, 1)
        minus = jnp.where((i1 + at == i2) & (j == k), jnp.float32(-1.0), 0.0)
        return jnp.where(j < PANELS, minus, x)

    def cut(ref, *index):
        return split(ref[index])

    def s1(at):
        rows = pl.ds(at, half)
        y0[rows, :] = unit(0, dot3(split(w[0, rows, :]), split(cross[0])), at)

    def s2(at):
        rows = pl.ds(at, half)
        y1[rows, :] = cross[1, rows, :] - dot3(split(u01[:, rows]), split(y0[...]), TN)

    def s3(at):
        rows = pl.ds(at, half)
        z0[rows, :] = dot3(split(w[0, :, rows]), split(y0[...]), TN)
        bt[rows, :] = dot3(split(w[0, :, rows]), split(u01[...]), TN)

    def s4(at):
        rows = pl.ds(at, half)
        y0[rows, :] = unit(1, dot3(split(w[1, rows, :]), split(y1[...])), at)

    def s5(at):
        rows = pl.ds(at, half)
        value = dot3(split(w[1, :, rows]), split(y0[...]), TN)
        top[1, rows, :], low[1, rows, :] = split(value)

    def s6(at):
        rows = pl.ds(at, half)
        value = z0[rows, :] - dot3(split(bt[rows, :]), (top[1], low[1]))
        top[0, rows, :], low[0, rows, :] = split(value)

    each_tile(s1, half)
    each_tile(s2, half)
    each_tile(s3, half)

    @pl.when(comm)
    def _():
        for b in range(n_dc):
            w_copy(1, b).wait_recv()

    each_tile(s4, half)
    each_tile(s5, half)
    each_tile(s6, half)

    @pl.when(chain)
    def _():
        def arrive(e, carry):
            x_copy(e // (2 * held), lax.rem(e // 2, held), lax.rem(e, 2), 2, dest(dd=sib)).wait_recv()
            return carry

        lax.fori_loop(0, PANELS * held * 2, arrive, 0)

    all_loads(True)

    def out_copy(s, h):
        rows = pl.ds(pl.multiple_of(h * half, half), half)
        return pltpu.make_async_copy(mbuf.at[s, rows, :], o_ref.at[s, rows, :], osend.at[s, h])

    def update(e, carry):
        a = e // 2
        h = lax.rem(e, 2)
        rows = pl.ds(pl.multiple_of(h * half, half), half)
        acc = jnp.where(j >= PANELS, mbuf[a + first, rows, :], 0.0)
        for k in range(PANELS):
            acc = acc - dot3(split(xs[k, a, rows, :]), (top[k], low[k]))
        mbuf[a + first, rows, :] = acc
        if first:
            out_copy(a + first, h).start()
        else:
            @pl.when((a > 0) | (r >= PANELS))
            def _():
                out_copy(a, h).start()
        return carry

    lax.fori_loop(0, 2 * held, update, 0)

    @pl.when(r < PANELS)
    def _():
        @pl.when(comm)
        def _():
            fix_copy().wait_recv()

        mbuf[0] = jnp.zeros((block, block), jnp.float32)

        def turned(ref):
            def turn(e, carry):
                i = pl.multiple_of((e // n_dc) * T, T)
                l = pl.multiple_of(lax.rem(e, n_dc) * T, T)
                mbuf[0, pl.ds(l, T), pl.ds(i, T)] = ref[pl.ds(i, T), pl.ds(l, T)].T
                return carry

            lax.fori_loop(0, n_dc * n_dc, turn, 0)

        @pl.when(j == r)
        def _():
            turned(ufix)

        @pl.when((j == 0) & (r == 1))
        def _():
            turned(u01)

        for h in range(2):
            out_copy(0, h).start()

    if first:
        pass

    @pl.when(r < PANELS)
    def _():
        for step in range(1, n_row):
            cross_copy(step).wait_send()

    @pl.when(chain)
    def _():
        for panel in range(PANELS):
            for b in range(n_dc):
                w_copy(panel, b).wait_send()
        u_copy().wait_send()

        @pl.when(r < PANELS)
        def _():
            fix_copy().wait_send()

    for n in range(len(DIAGS)):
        diag_drain(n)
    x_drain()

    def finish(e, carry):
        out_copy(e // 2, lax.rem(e, 2)).wait()
        return carry

    lax.fori_loop(0, 2 * slots, finish, 0)


def body(shape, matrix):
    n_row, n_col, n_dep = shape
    m = matrix.reshape(matrix.shape[0], matrix.shape[2], matrix.shape[3])
    slots, block, _ = m.shape
    first = 1 if n_row <= PANELS else 0
    held = slots - first
    n_dc = block // T
    n_pair = n_dep // 2
    f32 = jnp.float32
    dma = pltpu.SemaphoreType.DMA
    hbm = pl.BlockSpec(memory_space=pltpu.HBM)
    square = pltpu.VMEM((block, block), f32)
    out = pl.pallas_call(
        functools.partial(kernel, shape, first),
        out_shape=jax.ShapeDtypeStruct(m.shape, f32),
        in_specs=[hbm],
        out_specs=hbm,
        scratch_shapes=[
            pltpu.VMEM((PANELS, held, block, block), f32),
            pltpu.VMEM((slots, block, block), f32),
            pltpu.VMEM((len(DIAGS), block, block), f32),
            pltpu.VMEM((block, 2 * block), f32),
            pltpu.VMEM((T, 2 * T), f32),
            pltpu.VMEM((PANELS, block, block), f32),
            square, square,
            pltpu.VMEM((PANELS, block, block), f32),
            square, square, square, square,
            pltpu.VMEM((PANELS, block, block), jnp.bfloat16),
            pltpu.VMEM((PANELS, block, block), jnp.bfloat16),
            dma((len(DIAGS), n_dc + 1, n_pair + n_row)),
            dma((len(DIAGS), n_dc + 1)),
            dma((len(DIAGS), n_dc + 1)),
            dma((PANELS, held, 2, 2 + n_pair)),
            dma((PANELS, held, 2)),
            dma((n_row - 1,)),
            dma((PANELS,)),
            dma((1,)),
            dma((PANELS + 1, n_dc)),
            dma((PANELS + 1, n_dc)),
            dma((held,)),
            dma((slots, 2)),
        ],
        compiler_params=pltpu.CompilerParams(has_side_effects=True, vmem_limit_bytes=60 << 20),
    )(m)
    return out.reshape(matrix.shape)


def solution(mesh):
    shape = (mesh.shape["row"], mesh.shape["col"], mesh.shape["depth"])
    placed = P(None, "row", None, ("col", "depth"))
    return jax.shard_map(
        functools.partial(body, shape),
        mesh=mesh,
        in_specs=(placed,),
        out_specs=placed,
        check_vma=False,
    )
```

time: 361 us -> 214 us (0.59)
  the two profiles are of different devices: /device:TPU:28 before, /device:TPU:0 now
where the time goes in v1:
time: 214 us; the launch traced here: 213 us
  Pallas kernels  206 us (96%)
  local copies, waits for them, and re-layouts  7.76 us (4%)
    pallas_call x1, Pallas kernels, body(): pl.pallas_call(functools.partial(kernel, shape, first), out_shape=jax.Sha...  206 us
    unnamed x1, local copies, waits for them, and re-layouts  7.76 us

profile of v1, /device:TPU:0, one launch (start us, length us, event | category | flops | bytes accessed | tf_op | source)
XLA Modules:
  0.0 213.3 jit_solution(5558616884968214290)
XLA Ops:
  0.0 205.6 %shard_map.17 = f32[8,512,512]{2,1,0:T(8,128)} custom-call(f32[8,512,512]{2,1,0:T(8,128)} %bitcast.5), custom_call_target="tpu_custom_call" | custom-call | tf_op jit(solution)/shard_map/pallas_call | solution.py:575
  205.6 7.8 %copy.4 = f32[8,1,512,512]{3,2,1,0:T(8,128)} copy(f32[8,1,512,512]{3,2,1,0:T(8,128)} %bitcast.4) | data formatting | bytes 16777216

commit v2 on v1

--- a/solution.py
+++ b/solution.py
@@ -126,28 +126,49 @@
         entry = comm & near & (c == 0) & (r == row)
         out = [(0, comm & near & (c < n_col - 1), dest(cc=lax.rem(c + 1, n_col)))]
         for q in range(1, n_pair):
-            out.append((1 + q, comm & near, dest(dd=lax.rem(d + 2 * q, n_dep))))
+            out.append((1 + q, comm & near, dest(dd=lax.rem(sib + 2 * q, n_dep))))
         for step in range(1, n_row):
             rr = lax.rem(r + step, n_row)
             out.append((n_pair + step, entry, dest(rr=rr, dd=lax.rem(rr, 2))))
-        down = comm if own_entry else ((comm & jnp.logical_not(entry)) | root)
+        down = comm & near
+        if not own_entry:
+            down = (down & jnp.logical_not(entry)) | root
         out.insert(0, (1, down, dest(dd=sib)))
         rows = [x for x in out if x[0] > n_pair]
         rest = [x for x in out if x[0] <= n_pair]
         return root, rows + rest
 
+    def diag_early(n):
+        return DIAGS[n][0] % 2 == DIAGS[n][1] % 2
+
+    def diag_rows(n):
+        root, out = diag_roles(n)
+
+        @pl.when(root)
+        def _():
+            for g in range(len(chunks(n))):
+                diag_load(n, g).wait()
+                for lane, cond, to in out:
+                    if lane > n_pair:
+                        diag_copy(n, g, lane, to).start()
+
     def diag_step(n, g):
         root, out = diag_roles(n)
+        early = diag_early(n)
 
         @pl.when(root)
         def _():
-            diag_load(n, g).wait()
+            if not early:
+                diag_load(n, g).wait()
 
         @pl.when(jnp.logical_not(root))
         def _():
             diag_copy(n, g, 0, dest(dd=sib)).wait_recv()
 
         for lane, cond, to in out:
+            if early and lane > n_pair:
+                continue
+
             @pl.when(cond)
             def _():
                 diag_copy(n, g, lane, to).start()
@@ -176,7 +197,6 @@
     def cross_start():
         @pl.when(r < PANELS)
         def _():
-            cross_local().start()
             for step in range(1, n_row):
                 cross_copy(step).start()
 
@@ -200,17 +220,25 @@
         ok = comm & (cs >= 0) & (cs < n_col) & (lax.rem(col, n_row) == r) & (a >= first)
         return ok, jnp.clip(a - first, 0, held - 1)
 
-    def piece_out(s, side, step):
+    def along(direction):
         out = []
-        if step == 0:
-            if side == 1 or s == 0:
-                out.append((0, c < n_col - 1, dest(cc=lax.rem(c + 1, n_col))))
-            if side == -1 or s == 0:
-                out.append((1, c > 0, dest(cc=lax.rem(c + n_col - 1, n_col))))
-            for q in range(1, n_pair):
-                out.append((2 + q, c >= 0, dest(dd=lax.rem(d + 2 * q, n_dep))))
-        out.append((2, c >= 0, dest(dd=sib)))
+        for t in range(1, n_col):
+            cc = c + direction * t
+            lane = (t - 1) if direction > 0 else (n_col - 2 + t)
+            out.append((lane, (cc >= 0) & (cc < n_col), dest(cc=jnp.clip(cc, 0, n_col - 1))))
         return out
+
+    def pairs():
+        lane = 2 * (n_col - 1)
+        return [(lane + q, c >= 0, dest(dd=lax.rem(d + 2 * q, n_dep))) for q in range(1, n_pair)]
+
+    def down():
+        return [(2 * (n_col - 1), c >= 0, dest(dd=sib))]
+
+    def piece_out(s, step):
+        if step:
+            return down()
+        return pairs() + down() + (along(-1) + along(1) if s == 0 else [])
 
     def x_part(k, a, h):
         return xs.at[k, a, pl.ds(pl.multiple_of(h * half, half), half), :]
@@ -219,15 +247,16 @@
         part = x_part(k, a, h)
         return remote(part, part, xsend.at[k, a, h, lane], xrecv.at[k, a, h], to)
 
-    def x_event(s, side, step, k):
+    def x_event(s, side, step, k, out=None):
         ok, a = piece(s, side, step)
+        lanes = piece_out(s, step) if out is None else out
 
         @pl.when(ok)
         def _():
             def part(h, carry):
                 if s > 0 or step > 0:
-                    x_copy(k, a, h, 2, dest(dd=sib)).wait_recv()
-                for lane, cond, to in piece_out(s, side, step):
+                    x_copy(k, a, h, 0, dest(dd=sib)).wait_recv()
+                for lane, cond, to in lanes:
                     @pl.when(cond)
                     def _():
                         x_copy(k, a, h, lane, to).start()
@@ -257,7 +286,7 @@
             for s, side in places:
                 for step in range(n_pair):
                     ok, a = piece(s, side, step)
-                    for lane, cond, to in piece_out(s, side, step):
+                    for lane, cond, to in piece_out(s, step):
                         @pl.when(ok & cond)
                         def _():
                             x_copy(k, a, h, lane, to).wait_send()
@@ -319,22 +348,69 @@
 
     @pl.when(comm)
     def _():
-        diag_relay(0)
+        near = d < 2
+        far = jnp.logical_not(near)
+        head = near & (c == 0)
+        for n in range(len(DIAGS)):
+            if diag_early(n):
+                diag_rows(n)
+
+        @pl.when(r < PANELS)
+        def _():
+            cross_local().start()
+
+        source, _ = piece(0, 1, 0)
+
+        def own(kk):
+            k = lax.rem(r + kk, PANELS)
+
+            @pl.when(source)
+            def _():
+                cross_wait(k)
+            x_own(k)
+            x_event(0, 1, 0, k, down() + along(-1))
+
+        def others(kk):
+            x_event(0, 1, 0, lax.rem(r + kk, PANELS), pairs() + along(1))
+
+        @pl.when(jnp.logical_not(head))
+        def _():
+            own(0)
+
+        @pl.when(far)
+        def _():
+            others(0)
+
+        @pl.when(near)
+        def _():
+            for n in range(len(DIAGS)):
+                diag_relay(n)
+
+            @pl.when(head)
+            def _():
+                own(0)
+            others(0)
+
+        for kk in range(1, PANELS):
+            own(kk)
+            others(kk)
         cross_start()
+
+        all_loads(False)
         for kk in range(PANELS):
             k = lax.rem(r + kk, PANELS)
-            cross_wait(k)
-            x_own(k)
-            for step in range(n_pair):
-                x_event(0, 1, step, k)
-            diag_relay(1 + kk)
-        all_loads(False)
-        for s in range(1, n_col):
-            for kk in range(PANELS):
-                k = lax.rem(r + kk, PANELS)
-                for side in (1, -1):
-                    for step in range(n_pair):
-                        x_event(s, side, step, k)
+            for s, side in places[1:]:
+                x_event(s, side, 0, k)
+        for kk in range(PANELS):
+            k = lax.rem(r + kk, PANELS)
+            for s, side in places:
+                for step in range(1, n_pair):
+                    x_event(s, side, step, k)
+        @pl.when(jnp.logical_not(source))
+        def _():
+            for k in range(PANELS):
+                cross_wait(jnp.int32(k))
+
         for b in range(n_dc):
             w_copy(0, b).wait_recv()
         u_copy().wait_recv()
@@ -393,7 +469,16 @@
 
     @pl.when(chain)
     def _():
-        cross_start()
+        head = (d < 2) & (c == 0)
+
+        @pl.when(r < PANELS)
+        def _():
+            cross_local().start()
+
+        @pl.when(jnp.logical_not(head))
+        def _():
+            cross_start()
+
         diag_step(0, 0)
         work[pl.ds(0, T), pl.ds(0, T)] = diag[0, pl.ds(0, T), pl.ds(0, T)]
         all_loads(False)
@@ -404,6 +489,10 @@
             diag_relay(1)
 
         factor_block(0)
+
+        @pl.when(head)
+        def _():
+            cross_start()
 
         @pl.when(jnp.logical_not((r == diag_start[0]) & (c == 0) & (d == diag_start[1])))
         def _():
@@ -473,7 +562,7 @@
     @pl.when(chain)
     def _():
         def arrive(e, carry):
-            x_copy(e // (2 * held), lax.rem(e // 2, held), lax.rem(e, 2), 2, dest(dd=sib)).wait_recv()
+            x_copy(e // (2 * held), lax.rem(e // 2, held), lax.rem(e, 2), 0, dest(dd=sib)).wait_recv()
             return carry
 
         lax.fori_loop(0, PANELS * held * 2, arrive, 0)
@@ -592,7 +681,7 @@
             dma((len(DIAGS), n_dc + 1, n_pair + n_row)),
             dma((len(DIAGS), n_dc + 1)),
             dma((len(DIAGS), n_dc + 1)),
-            dma((PANELS, held, 2, 2 + n_pair)),
+            dma((PANELS, held, 2, 2 * (n_col - 1) + n_pair)),
             dma((PANELS, held, 2)),
             dma((n_row - 1,)),
             dma((PANELS,)),

time: 214 us -> 161 us (0.75)
  Pallas kernels: 206 us -> 152 us
    pallas_call x1, Pallas kernels: 206 us -> 152 us  [body(): pl.pallas_call(functools.partial(kernel, shape, first), out_shape=jax.Sha...]
where the time goes in v2:
time: 161 us; the launch traced here: 160 us
  Pallas kernels  152 us (94%)
  local copies, waits for them, and re-layouts  7.76 us (5%)
    pallas_call x1, Pallas kernels, body(): pl.pallas_call(functools.partial(kernel, shape, first), out_shape=jax.Sha...  152 us
    unnamed x1, local copies, waits for them, and re-layouts  7.76 us

profile of v2, /device:TPU:0, one launch (start us, length us, event | category | flops | bytes accessed | tf_op | source)
XLA Modules:
  0.0 160.2 jit_solution(6866730773715960756)
XLA Ops:
  0.0 152.4 %shard_map.17 = f32[8,512,512]{2,1,0:T(8,128)} custom-call(f32[8,512,512]{2,1,0:T(8,128)} %bitcast.5), custom_call_target="tpu_custom_call" | custom-call | tf_op jit(solution)/shard_map/pallas_call | solution.py:664
  152.4 7.8 %copy.4 = f32[8,1,512,512]{3,2,1,0:T(8,128)} copy(f32[8,1,512,512]{3,2,1,0:T(8,128)} %bitcast.4) | data formatting | bytes 16777216

commit v3 on v2

--- a/solution.py
+++ b/solution.py
@@ -11,6 +11,8 @@
 MESH = pl.DeviceIdType.MESH
 HI = lax.Precision.HIGHEST
 T = 128
+S = 16
+H = 4
 NT = (((1,), (1,)), ((), ()))
 TN = (((0,), (0,)), ((), ()))
 NN = (((1,), (0,)), ((), ()))
@@ -21,38 +23,73 @@
     return lax.dot_general(a, b, dims, precision=HI, preferred_element_type=jnp.float32)
 
 
+def stacked(x, order, axis):
+    top = x.astype(jnp.bfloat16)
+    rest = x - top.astype(jnp.float32)
+    mid = rest.astype(jnp.bfloat16)
+    low = (rest - mid.astype(jnp.float32)).astype(jnp.bfloat16)
+    parts = (top, mid, low)
+    return jnp.concatenate([parts[i] for i in order], axis=axis)
+
+
+def left6(x, axis):
+    return stacked(x, (1, 2, 0, 1, 0, 0), axis)
+
+
+def right6(x, axis=0):
+    return stacked(x, (1, 0, 2, 0, 1, 0), axis)
+
+
+def dot6(left, right, dims=NN):
+    return lax.dot_general(left, right, dims, preferred_element_type=jnp.float32)
+
+
 def factor_tile(aug):
+    n_part = S // 8
+
     def strip(i, carry):
-        j0 = pl.multiple_of(i * 8, 8)
-        rows = aug[pl.ds(j0, 8), :]
+        j0 = pl.multiple_of(i * S, S)
+        rows = [aug[pl.ds(j0 + 8 * p, 8), :] for p in range(n_part)]
         lane = lax.broadcasted_iota(jnp.int32, (8, T), 1)
         sub = lax.broadcasted_iota(jnp.int32, (8, T), 0)
         sub2 = lax.broadcasted_iota(jnp.int32, (8, 2 * T), 0)
-        left = rows[:, :T]
         cols = [
-            jnp.broadcast_to(
-                jnp.sum(jnp.where(lane == j0 + t, left, 0.0), axis=1, keepdims=True), (8, T)
-            )
-            for t in range(8)
+            [
+                jnp.broadcast_to(
+                    jnp.sum(jnp.where(lane == j0 + t, x[:, :T], 0.0), axis=1, keepdims=True), (8, T)
+                )
+                for t in range(S)
+            ]
+            for x in rows
         ]
-        for t in range(8):
-            p = cols[t][t : t + 1, :]
+        for t in range(S):
+            q, e = t // 8, t % 8
+            p = cols[q][t][e : e + 1, :]
             r = lax.rsqrt(p)
             r = r * (1.5 - 0.5 * p * r * r)
-            coef = cols[t] * r
-            for u in range(t + 1, 8):
-                head = cols[u][t : t + 1, :] * r
-                cols[u] = jnp.where(sub > t, cols[u] - coef * head, cols[u])
+            coef = {g: cols[g][t] * r for g in range(q, n_part)}
+            for u in range(t + 1, S):
+                head = cols[q][u][e : e + 1, :] * r
+                cols[q][u] = jnp.where(sub > e, cols[q][u] - coef[q] * head, cols[q][u])
+                for g in range(q + 1, n_part):
+                    cols[g][u] = cols[g][u] - coef[g] * head
             wide_r = jnp.concatenate([r, r], axis=1)
-            wide_c = jnp.concatenate([coef, coef], axis=1)
-            head = rows[t : t + 1, :] * wide_r
-            rows = jnp.where(sub2 == t, head, jnp.where(sub2 > t, rows - wide_c * head, rows))
-        aug[pl.ds(j0, 8), :] = rows
-        later = jnp.where(lane >= j0 + 8, rows[:, :T], 0.0)
-        aug[...] -= dot(later, rows, TN)
+            head = rows[q][e : e + 1, :] * wide_r
+            wide_c = jnp.concatenate([coef[q], coef[q]], axis=1)
+            rows[q] = jnp.where(
+                sub2 == e, head, jnp.where(sub2 > e, rows[q] - wide_c * head, rows[q])
+            )
+            for g in range(q + 1, n_part):
+                wide_c = jnp.concatenate([coef[g], coef[g]], axis=1)
+                rows[g] = rows[g] - wide_c * head
+        done = jnp.concatenate(rows, axis=0)
+        aug[pl.ds(j0, S), :] = done
+        wide = lax.broadcasted_iota(jnp.int32, (S, T), 1)
+        later = jnp.where(wide >= j0 + S, done[:, :T], 0.0)
+        aug[...] -= dot6(left6(later, 0), right6(done), TN)
         return carry
 
-    lax.fori_loop(0, T // 8, strip, 0)
+    lax.fori_loop(0, T // S, strip, 0)
 
 
 def split(x):
@@ -241,28 +278,49 @@
         return pairs() + down() + (along(-1) + along(1) if s == 0 else [])
 
     def x_part(k, a, h):
-        return xs.at[k, a, pl.ds(pl.multiple_of(h * half, half), half), :]
+        size = block // H
+        return xs.at[k, a, pl.ds(pl.multiple_of(h * size, size), size), :]
 
     def x_copy(k, a, h, lane, to):
         part = x_part(k, a, h)
         return remote(part, part, xsend.at[k, a, h, lane], xrecv.at[k, a, h], to)
 
-    def x_event(s, side, step, k, out=None):
-        ok, a = piece(s, side, step)
-        lanes = piece_out(s, step) if out is None else out
+    def x_send(k, out):
+        ok, a = piece(0, 1, 0)
 
         @pl.when(ok)
         def _():
             def part(h, carry):
-                if s > 0 or step > 0:
-                    x_copy(k, a, h, 0, dest(dd=sib)).wait_recv()
-                for lane, cond, to in lanes:
+                for lane, cond, to in out:
                     @pl.when(cond)
                     def _():
                         x_copy(k, a, h, lane, to).start()
                 return carry
 
-            lax.fori_loop(0, 2, part, 0)
+            lax.fori_loop(0, H, part, 0)
+
+    def x_event(s, side, step, k, h):
+        ok, a = piece(s, side, step)
+
+        @pl.when(ok)
+        def _():
+            x_copy(k, a, h, 0, dest(dd=sib)).wait_recv()
+            for lane, cond, to in piece_out(s, step):
+                x_copy(k, a, h, lane, to).start()
+
+    def turn_of(e):
+        return lax.rem(r + e // H, PANELS), lax.rem(e, H)
+
+    def x_line(e):
+        k, h = turn_of(e)
+        for s, side in places[1:]:
+            x_event(s, side, 0, k, h)
+
+    def x_across(e):
+        k, h = turn_of(e)
+        for s, side in places:
+            for step in range(1, n_pair):
+                x_event(s, side, step, k, h)
 
     places = [(0, 1)] + [(s, side) for s in range(1, n_col) for side in (1, -1)]
 
@@ -281,8 +339,8 @@
 
     def x_drain():
         def one(e, carry):
-            k = e // 2
-            h = lax.rem(e, 2)
+            k = e // H
+            h = lax.rem(e, H)
             for s, side in places:
                 for step in range(n_pair):
                     ok, a = piece(s, side, step)
@@ -292,7 +350,7 @@
                             x_copy(k, a, h, lane, to).wait_send()
             return carry
 
-        lax.fori_loop(0, 2 * PANELS, one, 0)
+        lax.fori_loop(0, H * PANELS, one, 0)
 
     def w_copy(panel, b):
         rows = pl.ds(pl.multiple_of(b * T, T), T)
@@ -345,6 +403,111 @@
             return carry
 
         lax.fori_loop(0, block // size, step, 0)
+
+    def unit(k, x, at):
+        i1 = lax.broadcasted_iota(jnp.int32, x.shape, 0)
+        i2 = lax.broadcasted_iota(jnp.int32, x.shape, 1)
+        minus = jnp.where((i1 + at == i2) & (j == k), jnp.float32(-1.0), 0.0)
+        return jnp.where(j < PANELS, minus, x)
+
+    def cut(ref, *index):
+        return split(ref[index])
+
+    def s1(at):
+        rows = pl.ds(at, half)
+        y0[rows, :] = unit(0, dot3(split(w[0, rows, :]), split(cross[0])), at)
+
+    def s2(at):
+        rows = pl.ds(at, half)
+        y1[rows, :] = cross[1, rows, :] - dot3(split(u01[:, rows]), split(y0[...]), TN)
+
+    def s3(at):
+        rows = pl.ds(at, half)
+        z0[rows, :] = dot3(split(w[0, :, rows]), split(y0[...]), TN)
+        bt[rows, :] = dot3(split(w[0, :, rows]), split(u01[...]), TN)
+
+    def early():
+        each_tile(s1, half)
+        each_tile(s2, half)
+        each_tile(s3, half)
+
+    def s4(at):
+        rows = pl.ds(at, half)
+        y0[rows, :] = unit(1, dot3(split(w[1, rows, :]), split(y1[...])), at)
+
+    def s5(at):
+        rows = pl.ds(at, half)
+        value = dot3(split(w[1, :, rows]), split(y0[...]), TN)
+        top[1, rows, :], low[1, rows, :] = split(value)
+
+    def s6(at):
+        rows = pl.ds(at, half)
+        value = z0[rows, :] - dot3(split(bt[rows, :]), (top[1], low[1]))
+        top[0, rows, :], low[0, rows, :] = split(value)
+
+    def middle():
+        each_tile(s4, half)
+        each_tile(s5, half)
+        each_tile(s6, half)
+
+    def out_copy(s, h):
+        rows = pl.ds(pl.multiple_of(h * (block // H), block // H), block // H)
+        return pltpu.make_async_copy(mbuf.at[s, rows, :], o_ref.at[s, rows, :], osend.at[s, h])
+
+    def update(h):
+        rows = pl.ds(pl.multiple_of(h * (block // H), block // H), block // H)
+
+        def one(a, carry):
+            acc = jnp.where(j >= PANELS, mbuf[a + first, rows, :], 0.0)
+            for k in range(PANELS):
+                acc = acc - dot3(split(xs[k, a, rows, :]), (top[k], low[k]))
+            if first:
+                mbuf[a + first, rows, :] = acc
+                out_copy(a + first, h).start()
+            else:
+                @pl.when((a > 0) | (r >= PANELS))
+                def _():
+                    mbuf[a, rows, :] = acc
+                    out_copy(a, h).start()
+            return carry
+
+        lax.fori_loop(0, held, one, 0)
+
+    def rest_of_update():
+        def one(h, carry):
+            update(h)
+            return carry
+
+        lax.fori_loop(2, H, one, 0)
+
+    def corner():
+        def turned(ref):
+            def turn(e, carry):
+                i = pl.multiple_of((e // n_dc) * T, T)
+                l = pl.multiple_of(lax.rem(e, n_dc) * T, T)
+                mbuf[0, pl.ds(l, T), pl.ds(i, T)] = ref[pl.ds(i, T), pl.ds(l, T)].T
+                return carry
+
+            lax.fori_loop(0, n_dc * n_dc, turn, 0)
+
+        @pl.when(r < PANELS)
+        def _():
+            @pl.when(comm)
+            def _():
+                fix_copy().wait_recv()
+
+            mbuf[0] = jnp.zeros((block, block), jnp.float32)
+
+            @pl.when(j == r)
+            def _():
+                turned(ufix)
+
+            @pl.when((j == 0) & (r == 1))
+            def _():
+                turned(u01)
+
+            for h in range(H):
+                out_copy(0, h).start()
 
     @pl.when(comm)
     def _():
@@ -368,10 +531,10 @@
             def _():
                 cross_wait(k)
             x_own(k)
-            x_event(0, 1, 0, k, down() + along(-1))
+            x_send(k, down() + along(-1))
 
         def others(kk):
-            x_event(0, 1, 0, lax.rem(r + kk, PANELS), pairs() + along(1))
+            x_send(lax.rem(r + kk, PANELS), pairs() + along(1))
 
         @pl.when(jnp.logical_not(head))
         def _():
@@ -397,23 +560,45 @@
         cross_start()
 
         all_loads(False)
-        for kk in range(PANELS):
-            k = lax.rem(r + kk, PANELS)
-            for s, side in places[1:]:
-                x_event(s, side, 0, k)
-        for kk in range(PANELS):
-            k = lax.rem(r + kk, PANELS)
-            for s, side in places:
-                for step in range(1, n_pair):
-                    x_event(s, side, step, k)
-        @pl.when(jnp.logical_not(source))
-        def _():
-            for k in range(PANELS):
-                cross_wait(jnp.int32(k))
-
+        n_event = PANELS * H
+        lead = n_event // 2
+
+        def first_part(e, carry):
+            x_line(e)
+            return carry
+
+        def second_part(e, carry):
+            @pl.when(e == lead // 2)
+            def _():
+                @pl.when(jnp.logical_not(source))
+                def _():
+                    for k in range(PANELS):
+                        cross_wait(jnp.int32(k))
+
+                for b in range(n_dc):
+                    w_copy(0, b).wait_recv()
+                u_copy().wait_recv()
+                early()
+
+            x_line(lead + e)
+
+            @pl.when(e > 0)
+            def _():
+                x_across(2 * e - 1)
+            x_across(2 * e)
+            return carry
+
+        lax.fori_loop(0, lead, first_part, 0)
+        lax.fori_loop(0, lead, second_part, 0)
         for b in range(n_dc):
-            w_copy(0, b).wait_recv()
-        u_copy().wait_recv()
+            w_copy(1, b).wait_recv()
+        middle()
+        all_loads(True)
+        corner()
+        update(0)
+        update(1)
+        x_across(n_event - 1)
+        rest_of_update()
 
     def factor_block(panel):
         def tile(b, carry):
@@ -428,7 +613,7 @@
                     for g in range(1, n_dc + 1):
                         diag_step(0, g)
                     each_tile(fill)
-            line = dot(aug[:, T:], work[rows, :])
+            line = dot6(left6(aug[:, T:], 1), right6(work[rows, :]))
             work[rows, :] = line
             w[panel, rows, :] = lower(line[:, block:], at)
 
@@ -441,12 +626,14 @@
                 lane = lax.broadcasted_iota(jnp.int32, (T, block), 1)
                 aside = jnp.where(lane >= at + T, line[:, :block], 0.0)
 
+                left = left6(aside, 0)
+
                 def tail(e, carry2):
                     cols = pl.ds(pl.multiple_of(e * 2 * T, 2 * T), 2 * T)
-                    work[:, cols] -= dot(aside, work[rows, cols], TN)
+                    work[:, cols] -= dot6(left, right6(work[rows, cols]), TN)
                     return carry2
 
-                lax.fori_loop(0, block // T, tail, 0)
+                lax.fori_loop((b + 1) // 2, block // (2 * T) + b // 2 + 1, tail, 0)
 
             w_copy(panel, b).start()
             return carry
@@ -510,117 +697,21 @@
         def _():
             fix_copy().start()
 
-    def unit(k, x, at):
-        i1 = lax.broadcasted_iota(jnp.int32, x.shape, 0)
-        i2 = lax.broadcasted_iota(jnp.int32, x.shape, 1)
-        minus = jnp.where((i1 + at == i2) & (j == k), jnp.float32(-1.0), 0.0)
-        return jnp.where(j < PANELS, minus, x)
-
-    def cut(ref, *index):
-        return split(ref[index])
-
-    def s1(at):
-        rows = pl.ds(at, half)
-        y0[rows, :] = unit(0, dot3(split(w[0, rows, :]), split(cross[0])), at)
-
-    def s2(at):
-        rows = pl.ds(at, half)
-        y1[rows, :] = cross[1, rows, :] - dot3(split(u01[:, rows]), split(y0[...]), TN)
-
-    def s3(at):
-        rows = pl.ds(at, half)
-        z0[rows, :] = dot3(split(w[0, :, rows]), split(y0[...]), TN)
-        bt[rows, :] = dot3(split(w[0, :, rows]), split(u01[...]), TN)
-
-    def s4(at):
-        rows = pl.ds(at, half)
-        y0[rows, :] = unit(1, dot3(split(w[1, rows, :]), split(y1[...])), at)
-
-    def s5(at):
-        rows = pl.ds(at, half)
-        value = dot3(split(w[1, :, rows]), split(y0[...]), TN)
-        top[1, rows, :], low[1, rows, :] = split(value)
-
-    def s6(at):
-        rows = pl.ds(at, half)
-        value = z0[rows, :] - dot3(split(bt[rows, :]), (top[1], low[1]))
-        top[0, rows, :], low[0, rows, :] = split(value)
-
-    each_tile(s1, half)
-    each_tile(s2, half)
-    each_tile(s3, half)
-
-    @pl.when(comm)
-    def _():
-        for b in range(n_dc):
-            w_copy(1, b).wait_recv()
-
-    each_tile(s4, half)
-    each_tile(s5, half)
-    each_tile(s6, half)
-
-    @pl.when(chain)
-    def _():
-        def arrive(e, carry):
-            x_copy(e // (2 * held), lax.rem(e // 2, held), lax.rem(e, 2), 0, dest(dd=sib)).wait_recv()
-            return carry
-
-        lax.fori_loop(0, PANELS * held * 2, arrive, 0)
-
-    all_loads(True)
-
-    def out_copy(s, h):
-        rows = pl.ds(pl.multiple_of(h * half, half), half)
-        return pltpu.make_async_copy(mbuf.at[s, rows, :], o_ref.at[s, rows, :], osend.at[s, h])
-
-    def update(e, carry):
-        a = e // 2
-        h = lax.rem(e, 2)
-        rows = pl.ds(pl.multiple_of(h * half, half), half)
-        acc = jnp.where(j >= PANELS, mbuf[a + first, rows, :], 0.0)
-        for k in range(PANELS):
-            acc = acc - dot3(split(xs[k, a, rows, :]), (top[k], low[k]))
-        mbuf[a + first, rows, :] = acc
-        if first:
-            out_copy(a + first, h).start()
-        else:
-            @pl.when((a > 0) | (r >= PANELS))
-            def _():
-                out_copy(a, h).start()
-        return carry
-
-    lax.fori_loop(0, 2 * held, update, 0)
-
-    @pl.when(r < PANELS)
-    def _():
-        @pl.when(comm)
-        def _():
-            fix_copy().wait_recv()
-
-        mbuf[0] = jnp.zeros((block, block), jnp.float32)
-
-        def turned(ref):
-            def turn(e, carry):
-                i = pl.multiple_of((e // n_dc) * T, T)
-                l = pl.multiple_of(lax.rem(e, n_dc) * T, T)
-                mbuf[0, pl.ds(l, T), pl.ds(i, T)] = ref[pl.ds(i, T), pl.ds(l, T)].T
-                return carry
-
-            lax.fori_loop(0, n_dc * n_dc, turn, 0)
-
-        @pl.when(j == r)
-        def _():
-            turned(ufix)
-
-        @pl.when((j == 0) & (r == 1))
-        def _():
-            turned(u01)
-
-        for h in range(2):
-            out_copy(0, h).start()
-
-    if first:
-        pass
+        early()
+        middle()
+        all_loads(True)
+        corner()
+
+        def last(h, carry):
+            def arrive(e, carry2):
+                x_copy(e // held, lax.rem(e, held), h, 0, dest(dd=sib)).wait_recv()
+                return carry2
+
+            lax.fori_loop(0, PANELS * held, arrive, 0)
+            update(h)
+            return carry
+
+        lax.fori_loop(0, H, last, 0)
 
     @pl.when(r < PANELS)
     def _():
@@ -643,10 +734,10 @@
     x_drain()
 
     def finish(e, carry):
-        out_copy(e // 2, lax.rem(e, 2)).wait()
+        out_copy(e // H, lax.rem(e, H)).wait()
         return carry
 
-    lax.fori_loop(0, 2 * slots, finish, 0)
+    lax.fori_loop(0, H * slots, finish, 0)
 
 
 def body(shape, matrix):
@@ -665,7 +756,7 @@
         functools.partial(kernel, shape, first),
         out_shape=jax.ShapeDtypeStruct(m.shape, f32),
         in_specs=[hbm],
-        out_specs=hbm,
+        out_specs=pl.BlockSpec(memory_space=pl.ANY),
         scratch_shapes=[
             pltpu.VMEM((PANELS, held, block, block), f32),
             pltpu.VMEM((slots, block, block), f32),
@@ -681,17 +772,17 @@
             dma((len(DIAGS), n_dc + 1, n_pair + n_row)),
             dma((len(DIAGS), n_dc + 1)),
             dma((len(DIAGS), n_dc + 1)),
-            dma((PANELS, held, 2, 2 * (n_col - 1) + n_pair)),
-            dma((PANELS, held, 2)),
+            dma((PANELS, held, H, 2 * (n_col - 1) + n_pair)),
+            dma((PANELS, held, H)),
             dma((n_row - 1,)),
             dma((PANELS,)),
             dma((1,)),
             dma((PANELS + 1, n_dc)),
             dma((PANELS + 1, n_dc)),
             dma((held,)),
-            dma((slots, 2)),
+            dma((slots, H)),
         ],
-        compiler_params=pltpu.CompilerParams(has_side_effects=True, vmem_limit_bytes=60 << 20),
+        compiler_params=pltpu.CompilerParams(has_side_effects=True, vmem_limit_bytes=44 << 20),
     )(m)
     return out.reshape(matrix.shape)
 

time: 161 us -> 148 us (0.919)
  Pallas kernels: 152 us -> 144 us
  local copies, waits for them, and re-layouts: 7.76 us -> 3.4 us
    pallas_call x1, Pallas kernels: 152 us -> 144 us  [body(): pl.pallas_call(functools.partial(kernel, shape, first), out_shape=jax.Sha...]
    unnamed x1, local copies, waits for them, and re-layouts: 7.76 us -> 3.4 us
where the time goes in v3:
time: 148 us; the launch traced here: 147 us
  Pallas kernels  144 us (97%)
  local copies, waits for them, and re-layouts  3.4 us (2%)
    pallas_call x1, Pallas kernels, body(): pl.pallas_call(functools.partial(kernel, shape, first), out_shape=jax.Sha...  144 us
    unnamed x1, local copies, waits for them, and re-layouts  3.4 us

profile of v3, /device:TPU:0, one launch (start us, length us, event | category | flops | bytes accessed | tf_op | source)
XLA Modules:
  0.0 147.4 jit_solution(8759347889143977570)
XLA Ops:
  0.0 144.0 %shard_map.17 = f32[8,512,512]{2,1,0:T(8,128)S(1)} custom-call(f32[8,512,512]{2,1,0:T(8,128)} %bitcast.5), custom_call_target="tpu_custom_call" | custom-call | tf_op jit(solution)/shard_map/pallas_call | solution.py:755
  144.0 3.4 %copy.4 = f32[8,1,512,512]{3,2,1,0:T(8,128)} copy(f32[8,1,512,512]{3,2,1,0:T(8,128)S(1)} %bitcast.4) | data formatting | bytes 16777216

commit v4 on v3

--- a/solution.py
+++ b/solution.py
@@ -546,16 +546,23 @@
 
         @pl.when(near)
         def _():
-            for n in range(len(DIAGS)):
-                diag_relay(n)
+            diag_relay(0)
+            diag_relay(1)
 
             @pl.when(head)
             def _():
                 own(0)
-            others(0)
+            x_send(lax.rem(r, PANELS), pairs())
 
         for kk in range(1, PANELS):
             own(kk)
+
+        @pl.when(near)
+        def _():
+            diag_relay(2)
+            x_send(lax.rem(r, PANELS), along(1))
+
+        for kk in range(1, PANELS):
             others(kk)
         cross_start()
 
@@ -580,6 +587,15 @@
                 u_copy().wait_recv()
                 early()
 
+            @pl.when(e == lead - 1)
+            def _():
+                for b in range(n_dc):
+                    w_copy(1, b).wait_recv()
+                middle()
+                all_loads(True)
+                corner()
+                update(0)
+
             x_line(lead + e)
 
             @pl.when(e > 0)
@@ -590,12 +606,6 @@
 
         lax.fori_loop(0, lead, first_part, 0)
         lax.fori_loop(0, lead, second_part, 0)
-        for b in range(n_dc):
-            w_copy(1, b).wait_recv()
-        middle()
-        all_loads(True)
-        corner()
-        update(0)
         update(1)
         x_across(n_event - 1)
         rest_of_update()

time: 148 us -> 142 us (0.959)
  Pallas kernels: 144 us -> 138 us
    pallas_call x1, Pallas kernels: 144 us -> 138 us  [body(): pl.pallas_call(functools.partial(kernel, shape, first), out_shape=jax.Sha...]
where the time goes in v4:
time: 142 us
  Pallas kernels  138 us (97%)
  local copies, waits for them, and re-layouts  3.4 us (2%)
    pallas_call x1, Pallas kernels, body(): pl.pallas_call(functools.partial(kernel, shape, first), out_shape=jax.Sha...  138 us
    unnamed x1, local copies, waits for them, and re-layouts  3.4 us

profile of v4, /device:TPU:0, one launch (start us, length us, event | category | flops | bytes accessed | tf_op | source)
XLA Modules:
  0.0 141.7 jit_solution(9962711039420643237)
XLA Ops:
  0.0 138.3 %shard_map.17 = f32[8,512,512]{2,1,0:T(8,128)S(1)} custom-call(f32[8,512,512]{2,1,0:T(8,128)} %bitcast.5), custom_call_target="tpu_custom_call" | custom-call | tf_op jit(solution)/shard_map/pallas_call | solution.py:765
  138.3 3.4 %copy.4 = f32[8,1,512,512]{3,2,1,0:T(8,128)} copy(f32[8,1,512,512]{3,2,1,0:T(8,128)S(1)} %bitcast.4) | data formatting | bytes 16777216

commit v5 on v4

--- a/solution.py
+++ b/solution.py
@@ -478,7 +478,7 @@
             update(h)
             return carry
 
-        lax.fori_loop(2, H, one, 0)
+        lax.fori_loop(3, H, one, 0)
 
     def corner():
         def turned(ref):
@@ -587,6 +587,10 @@
                 u_copy().wait_recv()
                 early()
 
+            @pl.when(e > 0)
+            def _():
+                x_across(2 * e - 1)
+
             @pl.when(e == lead - 1)
             def _():
                 for b in range(n_dc):
@@ -595,18 +599,15 @@
                 all_loads(True)
                 corner()
                 update(0)
+                update(1)
 
             x_line(lead + e)
-
-            @pl.when(e > 0)
-            def _():
-                x_across(2 * e - 1)
             x_across(2 * e)
             return carry
 
         lax.fori_loop(0, lead, first_part, 0)
         lax.fori_loop(0, lead, second_part, 0)
-        update(1)
+        update(2)
         x_across(n_event - 1)
         rest_of_update()
 

time: 142 us -> 146 us (1.028); the launches traced: 142 us -> 144 us
  Pallas kernels: 138 us -> 140 us
    pallas_call x1, Pallas kernels: 138 us -> 140 us  [body(): pl.pallas_call(functools.partial(kernel, shape, first), out_shape=jax.Sha...]
where the time goes in v5:
time: 146 us; the launch traced here: 144 us
  Pallas kernels  140 us (96%)
  local copies, waits for them, and re-layouts  3.4 us (2%)
    pallas_call x1, Pallas kernels, body(): pl.pallas_call(functools.partial(kernel, shape, first), out_shape=jax.Sha...  140 us
    unnamed x1, local copies, waits for them, and re-layouts  3.4 us

profile of v5, /device:TPU:0, one launch (start us, length us, event | category | flops | bytes accessed | tf_op | source)
XLA Modules:
  0.0 143.6 jit_solution(12050578908960153475)
XLA Ops:
  0.0 140.2 %shard_map.17 = f32[8,512,512]{2,1,0:T(8,128)S(1)} custom-call(f32[8,512,512]{2,1,0:T(8,128)} %bitcast.5), custom_call_target="tpu_custom_call" | custom-call | tf_op jit(solution)/shard_map/pallas_call | solution.py:766
  140.2 3.4 %copy.4 = f32[8,1,512,512]{3,2,1,0:T(8,128)} copy(f32[8,1,512,512]{3,2,1,0:T(8,128)S(1)} %bitcast.4) | data formatting | bytes 16777216
